TPU v7x, 32 devices: a whole 2x2x4 slice. The times are simulated.
32 devices in a mesh: slab: 2 (over x), row: 8 (over z, y), col: 2 (over core).
Axes of the slice: x: 2, y: 2, z: 4, core: 2. Of those that a mesh axis runs over, the one named last changes fastest.
Arguments:
- image: float32 [1024, 4096], P(('slab', 'row'), 'col'), parts along dimension 0, may hold values from -6 to 6
Outputs:
- dog_fine: bfloat16 [4, 1024, 4096], P(None, ('slab', 'row'), 'col'), parts along dimension 1
- hessian_fine: bfloat16 [2, 1024, 4096], P(None, ('slab', 'row'), 'col'), parts along dimension 1
- dog_coarse: bfloat16 [4, 512, 2048], P(None, ('slab', 'row', 'col')), parts along dimension 1
- hessian_coarse: bfloat16 [2, 512, 2048], P(None, ('slab', 'row', 'col')), parts along dimension 1
There are 2 independent parts, one for each index of `slab`. A program takes and returns all parts, laid end to end along the dimension named above; each array names one. Nothing has to cross between parts.
All inputs are finite; a program needn't handle non-finite values.
Results may differ from a plain program's by a relative error of at most 0.0013.
Values may be sent and summed in bfloat16 or wider, within the bound.
A program may use at most 64 MiB of HBM per device.

v0:
```python
import jax
import jax.numpy as jnp
from jax import lax
from jax.sharding import PartitionSpec as P

SIGMAS = [1.6 * 2.0 ** (k / 4.0) for k in range(5)]


def with_halo(x, sides, width):
    for axis, dim in sides:
        devices, length = (lax.axis_size(axis), x.shape[dim])
        up = [(i, (i + 1) % devices) for i in range(devices - 1)]
        down = [(j, i) for i, j in up]
        last = lax.slice_in_dim(x, length - width, length, axis=dim)
        first = lax.slice_in_dim(x, 0, width, axis=dim)
        before = lax.ppermute(last, axis, up)
        after = lax.ppermute(first, axis, down)
        x = jnp.concatenate([before, x, after], axis=dim)
    return x


def band(sigma, count_out, count_in, offset):
    outer = jnp.arange(count_out)[:, None]
    inner = jnp.arange(count_in)[None, :]
    diff = inner - outer + offset
    spread = jnp.arange(25).astype(jnp.float32) - 12.0
    total = jnp.sum(jnp.exp(-spread * spread / (2.0 * sigma * sigma)))
    centred = diff.astype(jnp.float32) - 12.0
    weights = jnp.exp(-centred * centred / (2.0 * sigma * sigma)) / total
    return jnp.where((diff >= 0) & (diff <= 24), weights, 0.0)


def vertical(field, sigma):
    count = field.shape[0]
    matrix = band(sigma, count - 24, count, 0)
    return jnp.dot(matrix, field, precision=lax.Precision.HIGHEST)


def horizontal(field, sigma):
    length = field.shape[1]
    out_len = length - 24
    blocks = -(-out_len // 128)
    padded = jnp.pad(field, ((0, 0), (0, (blocks + 1) * 128 - length)))
    tiles = padded.reshape(field.shape[0], blocks + 1, 128)
    main = band(sigma, 128, 128, 0)
    carry = band(sigma, 128, 128, 128)
    result = jnp.einsum("rbi,oi->rbo", tiles[:, :blocks], main, precision=lax.Precision.HIGHEST)
    result = result + jnp.einsum(
        "rbi,oi->rbo", tiles[:, 1:], carry, precision=lax.Precision.HIGHEST
    )
    return result.reshape(field.shape[0], blocks * 128)[:, :out_len]


def hessian_valid(padded):
    centre = padded[:, 1:-1, 1:-1]
    dxx = padded[:, 1:-1, 2:] + padded[:, 1:-1, :-2] - 2.0 * centre
    dyy = padded[:, 2:, 1:-1] + padded[:, :-2, 1:-1] - 2.0 * centre
    dxy = (padded[:, 2:, 2:] - padded[:, 2:, :-2] - padded[:, :-2, 2:] + padded[:, :-2, :-2]) / 4.0
    return dxx * dyy - dxy * dxy


def scale_space(extended, spare, row_start, col_start, height, width, dog_gain, hess_gain):
    rows = extended.shape[0] - 24 - 2 * spare
    cols = extended.shape[1] - 24 - 2 * spare
    levels = [horizontal(vertical(extended, s), s) for s in SIGMAS]
    diffs = [levels[k + 1] - levels[k] for k in range(4)]
    dogs = jnp.stack(
        [
            (dog_gain * d[spare : spare + rows, spare : spare + cols]).astype(jnp.bfloat16)
            for d in diffs
        ]
    )
    middle = jnp.stack([diffs[1], diffs[2]])
    row_pos = row_start - 1 + jnp.arange(rows + 2)
    col_pos = col_start - 1 + jnp.arange(cols + 2)
    inside = ((row_pos >= 0) & (row_pos < height))[:, None] & ((col_pos >= 0) & (col_pos < width))[
        None, :
    ]
    padded = middle * inside.astype(jnp.float32)[None]
    hess = (hess_gain * hessian_valid(padded)).astype(jnp.bfloat16)
    return (dogs, hess, levels[4][spare : spare + rows, spare : spare + cols])


def local(image):
    tile_rows, tile_cols = image.shape
    spare = 1
    reach = 12 + spare
    height = tile_rows * lax.axis_size("row")
    width = tile_cols * lax.axis_size("col")
    extended = with_halo(image, (("row", 0), ("col", 1)), reach)
    dog_fine, hessian_fine, top_level = scale_space(
        extended,
        spare,
        lax.axis_index("row") * tile_rows,
        lax.axis_index("col") * tile_cols,
        height,
        width,
        20.0,
        5000.0,
    )
    coarse_base = top_level[0::2, 0::2]
    grown = with_halo(coarse_base, (("row", 0), ("col", 1)), reach)
    dog_tile, hess_tile, unused = scale_space(
        grown,
        spare,
        lax.axis_index("row") * coarse_base.shape[0],
        lax.axis_index("col") * coarse_base.shape[1],
        height // 2,
        width // 2,
        80.0,
        200000.0,
    )
    stacked = jnp.concatenate([dog_tile, hess_tile], axis=0)
    relaid = lax.all_to_all(stacked, "col", split_axis=1, concat_axis=2, tiled=True)
    dog_coarse = relaid[:4]
    hessian_coarse = relaid[4:]
    return (dog_fine, hessian_fine, dog_coarse, hessian_coarse)


def solution(mesh):
    return jax.shard_map(
        local,
        mesh=mesh,
        in_specs=(P(("slab", "row"), "col"),),
        out_specs=(
            P(None, ("slab", "row"), "col"),
            P(None, ("slab", "row"), "col"),
            P(None, ("slab", "row", "col"), None),
            P(None, ("slab", "row", "col"), None),
        ),
        check_vma=False,
    )
```

profile of v0, /device:TPU:14, one launch (start us, length us, event | category | flops | bytes accessed | tf_op | source)
XLA Modules:
  0.0 98.3 jit_solution(10586258024756835656)
XLA Ops:
  1.7 2.4 %collective-permute-start.1 = (f32[13,2048]{1,0:T(8,128)S(1)}, f32[13,2048]{1,0:T(8,128)S(1)}, u32[]{:S(2)}, u32[]{:S(2)}) collective-permute-start(f32[13,2048]{1,0:T(8,128)S(1)} %get-tuple-element.21), channel_id=1, source_target_pairs={{2,0},{4,2},{6,4},{8,6},{10,8},{12,10},{14,12},{3,1},{5,3},{7,5},{... | collective-permute-start | bytes 319496 | tf_op jit(solution)/shard_map/ppermute | solution.py:17
  4.1 4.3 %collective-permute-start = (f32[13,2048]{1,0:T(8,128)S(1)}, f32[13,2048]{1,0:T(8,128)S(1)}, u32[]{:S(2)}, u32[]{:S(2)}) collective-permute-start(f32[13,2048]{1,0:T(8,128)S(1)} %get-tuple-element.20), channel_id=1, source_target_pairs={{0,2},{2,4},{4,6},{6,8},{8,10},{10,12},{12,14},{1,3},{3,5},{5,7},{... | collective-permute-start | bytes 319496 | tf_op jit(solution)/shard_map/ppermute | solution.py:16
  9.8 2.7 %collective-permute-done = f32[13,2048]{1,0:T(8,128)S(1)} collective-permute-done((f32[13,2048]{1,0:T(8,128)S(1)}, f32[13,2048]{1,0:T(8,128)S(1)}, u32[]{:S(2)}, u32[]{:S(2)}) %collective-permute-start) | collective-permute-done | bytes 106528 | tf_op jit(solution)/shard_map/ppermute | solution.py:16
  12.7 1.9 %collective-permute-start.2 = (f32[90,13]{1,0:T(8,128)S(1)}, f32[90,13]{1,0:T(8,128)S(1)}, u32[]{:S(2)}, u32[]{:S(2)}) collective-permute-start(f32[90,13]{1,0:T(8,128)S(1)} %get-tuple-element.15), channel_id=1, source_target_pairs={{0,1},{2,3},{4,5},{6,7},{8,9},{10,11},{12,13},{14,15},{16,17},{18,... | collective-permute-start | bytes 14048 | tf_op jit(solution)/shard_map/ppermute | solution.py:16
  19.5 1.4 %fusion.118 = f32[66,2074]{1,0:T(8,128)S(1)} fusion(f32[90,2074]{1,0:T(8,128)S(1)} %concatenate.16, f32[]{:T(128)} %exponential_reduce_fusion.4), kind=kOutput, calls=%fused_computation.175 | convolution fusion | flops 147900064 | bytes 1294180 | tf_op jit(solution)/shard_map/dot_general | solution.py:36
  21.2 1.8 %fusion.21 = f32[66,17,128]{2,0,1:T(8,128)S(1)} fusion(f32[66,17,128]{2,1,0:T(8,128)S(1)} %get-tuple-element.7, f32[]{:T(128)} %exponential_reduce_fusion.4), kind=kOutput, calls=%fused_computation.40 | convolution fusion | flops 220774400 | bytes 1148932 | tf_op jit(solution)/shard_map/rbi,oi->rbo/dot_general | solution.py:47
  23.0 1.8 %convolution_add_fusion.4 = f32[66,17,128]{2,0,1:T(8,128)S(1)} fusion(f32[66,17,128]{2,0,1:T(8,128)S(1)} %fusion.21, f32[66,17,128]{2,1,0:T(8,128)S(1)} %get-tuple-element.6, f32[]{:T(128)} %exponential_reduce_fusion.4), kind=kOutput, calls=%fused_computation.4 | convolution fusion | flops 220934400 | bytes 1723396 | tf_op jit(solution)/shard_map/rbi,oi->rbo/dot_general | solution.py:48
  26.0 1.4 %fusion.108 = f32[66,2074]{1,0:T(8,128)S(1)} fusion(f32[90,2074]{1,0:T(8,128)S(1)} %concatenate.16, f32[]{:T(128)} %exponential_reduce_fusion.2), kind=kOutput, calls=%fused_computation.165 | convolution fusion | flops 147900064 | bytes 1294180 | tf_op jit(solution)/shard_map/dot_general | solution.py:36
  27.6 1.8 %fusion.15 = f32[66,17,128]{2,0,1:T(8,128)S(1)} fusion(f32[66,17,128]{2,1,0:T(8,128)S(1)} %get-tuple-element.9, f32[]{:T(128)} %exponential_reduce_fusion.2), kind=kOutput, calls=%fused_computation.34 | convolution fusion | flops 220774400 | bytes 1148932 | tf_op jit(solution)/shard_map/rbi,oi->rbo/dot_general | solution.py:47
  29.5 1.8 %convolution_add_fusion.2 = f32[66,17,128]{2,0,1:T(8,128)S(1)} fusion(f32[66,17,128]{2,0,1:T(8,128)S(1)} %fusion.15, f32[66,17,128]{2,1,0:T(8,128)S(1)} %get-tuple-element.8, f32[]{:T(128)} %exponential_reduce_fusion.2), kind=kOutput, calls=%fused_computation.2 | convolution fusion | flops 220934400 | bytes 1723396 | tf_op jit(solution)/shard_map/rbi,oi->rbo/dot_general | solution.py:48
  32.4 1.4 %fusion.103 = f32[66,2074]{1,0:T(8,128)S(1)} fusion(f32[90,2074]{1,0:T(8,128)S(1)} %concatenate.16, f32[]{:T(128)} %exponential_reduce_fusion.1), kind=kOutput, calls=%fused_computation.160 | convolution fusion | flops 147900064 | bytes 1294180 | tf_op jit(solution)/shard_map/dot_general | solution.py:36
  34.1 1.8 %fusion.12 = f32[66,17,128]{2,0,1:T(8,128)S(1)} fusion(f32[66,17,128]{2,1,0:T(8,128)S(1)} %get-tuple-element.13, f32[]{:T(128)} %exponential_reduce_fusion.1), kind=kOutput, calls=%fused_computation.31 | convolution fusion | flops 220774400 | bytes 1148932 | tf_op jit(solution)/shard_map/rbi,oi->rbo/dot_general | solution.py:47
  35.9 1.8 %convolution_add_fusion.1 = f32[66,17,128]{2,0,1:T(8,128)S(1)} fusion(f32[66,17,128]{2,0,1:T(8,128)S(1)} %fusion.12, f32[66,17,128]{2,1,0:T(8,128)S(1)} %get-tuple-element.12, f32[]{:T(128)} %exponential_reduce_fusion.1), kind=kOutput, calls=%fused_computation.1 | convolution fusion | flops 220934400 | bytes 1723396 | tf_op jit(solution)/shard_map/rbi,oi->rbo/dot_general | solution.py:48
  40.4 1.9 %fusion.9 = f32[66,17,128]{2,0,1:T(8,128)S(1)} fusion(f32[66,17,128]{2,1,0:T(8,128)S(1)} %get-tuple-element.11, f32[]{:T(128)} %exponential_reduce_fusion), kind=kOutput, calls=%fused_computation.28 | convolution fusion | flops 220774400 | bytes 1148932 | tf_op jit(solution)/shard_map/rbi,oi->rbo/dot_general | solution.py:47
  42.3 1.7 %convolution_add_fusion = f32[66,17,128]{2,0,1:T(8,128)S(1)} fusion(f32[66,17,128]{2,0,1:T(8,128)S(1)} %fusion.9, f32[66,17,128]{2,1,0:T(8,128)S(1)} %get-tuple-element.10, f32[]{:T(128)} %exponential_reduce_fusion), kind=kOutput, calls=%fused_computation | convolution fusion | flops 220934400 | bytes 1723396 | tf_op jit(solution)/shard_map/rbi,oi->rbo/dot_general | solution.py:48
  44.4 1.4 %fusion.113 = f32[66,2074]{1,0:T(8,128)S(1)} fusion(f32[90,2074]{1,0:T(8,128)S(1)} %concatenate.16, f32[]{:T(128)} %exponential_reduce_fusion.3), kind=kOutput, calls=%fused_computation.170 | convolution fusion | flops 147900064 | bytes 1294180 | tf_op jit(solution)/shard_map/dot_general | solution.py:36
  46.1 1.8 %fusion.18 = f32[66,17,128]{2,0,1:T(8,128)S(1)} fusion(f32[66,17,128]{2,1,0:T(8,128)S(1)} %get-tuple-element.5, f32[]{:T(128)} %exponential_reduce_fusion.3), kind=kOutput, calls=%fused_computation.37 | convolution fusion | flops 220774400 | bytes 1148932 | tf_op jit(solution)/shard_map/rbi,oi->rbo/dot_general | solution.py:47
  47.9 1.8 %convolution_add_fusion.3 = f32[66,17,128]{2,0,1:T(8,128)S(1)} fusion(f32[66,17,128]{2,0,1:T(8,128)S(1)} %fusion.18, f32[66,17,128]{2,1,0:T(8,128)S(1)} %get-tuple-element.4, f32[]{:T(128)} %exponential_reduce_fusion.3), kind=kOutput, calls=%fused_computation.3 | convolution fusion | flops 220934400 | bytes 1723396 | tf_op jit(solution)/shard_map/rbi,oi->rbo/dot_general | solution.py:48
  51.1 4.4 %slice.244 = f32[32,1024]{1,0:T(8,128)S(1)} slice(f32[64,2048]{1,0:T(8,128)S(1)} %slice.313), slice={[0:64:2], [0:2048:2]} | slice | bytes 262144 | tf_op jit(solution)/shard_map/slice | solution.py:101
  55.6 2.0 %collective-permute-start.5 = (f32[13,1024]{1,0:T(8,128)S(1)}, f32[13,1024]{1,0:T(8,128)S(1)}, u32[]{:S(2)}, u32[]{:S(2)}) collective-permute-start(f32[13,1024]{1,0:T(8,128)S(1)} %get-tuple-element.39), channel_id=1, source_target_pairs={{2,0},{4,2},{6,4},{8,6},{10,8},{12,10},{14,12},{3,1},{5,3},{7,5},{... | collective-permute-start | bytes 159752 | tf_op jit(solution)/shard_map/ppermute | solution.py:17
  57.6 4.9 %collective-permute-start.4 = (f32[13,1024]{1,0:T(8,128)S(1)}, f32[13,1024]{1,0:T(8,128)S(1)}, u32[]{:S(2)}, u32[]{:S(2)}) collective-permute-start(f32[13,1024]{1,0:T(8,128)S(1)} %get-tuple-element.38), channel_id=1, source_target_pairs={{0,2},{2,4},{4,6},{6,8},{8,10},{10,12},{12,14},{1,3},{3,5},{5,7},{... | collective-permute-start | bytes 159752 | tf_op jit(solution)/shard_map/ppermute | solution.py:16
  65.6 2.5 %fusion.4 = bf16[2,64,2048]{2,1,0:T(8,128)(2,1)} fusion(f32[2,66,2050]{2,1,0:T(8,128)S(1)} %maximum_multiply_fusion), kind=kLoop, calls=%fused_computation.16 | loop fusion | flops 3670016 | bytes 9961472 | tf_op jit(solution)/shard_map/convert_element_type | solution.py:80
  68.2 2.5 %collective-permute-start.6 = (f32[58,13]{1,0:T(8,128)S(1)}, f32[58,13]{1,0:T(8,128)S(1)}, u32[]{:S(2)}, u32[]{:S(2)}) collective-permute-start(f32[58,13]{1,0:T(8,128)S(1)} %get-tuple-element.33), channel_id=1, source_target_pairs={{0,1},{2,3},{4,5},{6,7},{8,9},{10,11},{12,13},{14,15},{16,17},{18,... | collective-permute-start | bytes 9056 | tf_op jit(solution)/shard_map/ppermute | solution.py:16
  92.5 4.2 %all_to_all.15 = bf16[6,32,1024]{2,0,1:T(8,128)(2,1)S(1)} all-to-all(bf16[6,32,1024]{2,0,1:T(8,128)(2,1)S(1)} %copy.117), channel_id=1, replica_groups=mesh['slab'=2,'row'=8,'col'=2] {'col'}, dimensions={1} | all-to-all | bytes 786432 | tf_op jit(solution)/shard_map/all_to_all | solution.py:114
  (131 shorter events, 41.3 us)
Async XLA Ops:
  0.6 11.9 %copy-start.3 = (f32[64,2048]{1,0:T(8,128)S(1)}, f32[64,2048]{1,0:T(8,128)}, u32[]{:S(2)}) copy-start(f32[64,2048]{1,0:T(8,128)} %param.1) | copy-start | bytes 1572868
  1.7 8.1 %collective-permute-start.1 = (f32[13,2048]{1,0:T(8,128)S(1)}, f32[13,2048]{1,0:T(8,128)S(1)}, u32[]{:S(2)}, u32[]{:S(2)}) collective-permute-start(f32[13,2048]{1,0:T(8,128)S(1)} %get-tuple-element.21), channel_id=1, source_target_pairs={{2,0},{4,2},{6,4},{8,6},{10,8},{12,10},{14,12},{3,1},{5,3},{7,5},{... | collective-permute-start | bytes 319496 | tf_op jit(solution)/shard_map/ppermute | solution.py:17
  4.1 8.4 %collective-permute-start = (f32[13,2048]{1,0:T(8,128)S(1)}, f32[13,2048]{1,0:T(8,128)S(1)}, u32[]{:S(2)}, u32[]{:S(2)}) collective-permute-start(f32[13,2048]{1,0:T(8,128)S(1)} %get-tuple-element.20), channel_id=1, source_target_pairs={{0,2},{2,4},{4,6},{6,8},{8,10},{10,12},{12,14},{1,3},{3,5},{5,7},{... | collective-permute-start | bytes 319496 | tf_op jit(solution)/shard_map/ppermute | solution.py:16
  12.7 6.5 %collective-permute-start.2 = (f32[90,13]{1,0:T(8,128)S(1)}, f32[90,13]{1,0:T(8,128)S(1)}, u32[]{:S(2)}, u32[]{:S(2)}) collective-permute-start(f32[90,13]{1,0:T(8,128)S(1)} %get-tuple-element.15), channel_id=1, source_target_pairs={{0,1},{2,3},{4,5},{6,7},{8,9},{10,11},{12,13},{14,15},{16,17},{18,... | collective-permute-start | bytes 14048 | tf_op jit(solution)/shard_map/ppermute | solution.py:16
  14.6 4.5 %collective-permute-start.3 = (f32[90,13]{1,0:T(8,128)S(1)}, f32[90,13]{1,0:T(8,128)S(1)}, u32[]{:S(2)}, u32[]{:S(2)}) collective-permute-start(f32[90,13]{1,0:T(8,128)S(1)} %get-tuple-element.14), channel_id=1, source_target_pairs={{1,0},{3,2},{5,4},{7,6},{9,8},{11,10},{13,12},{15,14},{17,16},{19,... | collective-permute-start | bytes 14048 | tf_op jit(solution)/shard_map/ppermute | solution.py:17
  50.0 12.6 %copy-start = (f32[9,8,17,128]{3,1,2,0:T(8,128)S(1)}, f32[9,8,17,128]{3,1,2,0:T(8,128)}, u32[]{:S(2)}) copy-start(f32[9,8,17,128]{3,1,2,0:T(8,128)} %copy.143) | copy-start | bytes 1880068
  50.0 12.6 %copy-start.1 = (f32[9,8,17,128]{3,1,2,0:T(8,128)S(1)}, f32[9,8,17,128]{3,1,2,0:T(8,128)}, u32[]{:S(2)}) copy-start(f32[9,8,17,128]{3,1,2,0:T(8,128)} %copy.145) | copy-start | bytes 1880068
  55.6 12.5 %collective-permute-start.5 = (f32[13,1024]{1,0:T(8,128)S(1)}, f32[13,1024]{1,0:T(8,128)S(1)}, u32[]{:S(2)}, u32[]{:S(2)}) collective-permute-start(f32[13,1024]{1,0:T(8,128)S(1)} %get-tuple-element.39), channel_id=1, source_target_pairs={{2,0},{4,2},{6,4},{8,6},{10,8},{12,10},{14,12},{3,1},{5,3},{7,5},{... | collective-permute-start | bytes 159752 | tf_op jit(solution)/shard_map/ppermute | solution.py:17
  57.6 10.5 %collective-permute-start.4 = (f32[13,1024]{1,0:T(8,128)S(1)}, f32[13,1024]{1,0:T(8,128)S(1)}, u32[]{:S(2)}, u32[]{:S(2)}) collective-permute-start(f32[13,1024]{1,0:T(8,128)S(1)} %get-tuple-element.38), channel_id=1, source_target_pairs={{0,2},{2,4},{4,6},{6,8},{8,10},{10,12},{12,14},{1,3},{3,5},{5,7},{... | collective-permute-start | bytes 159752 | tf_op jit(solution)/shard_map/ppermute | solution.py:16
  63.8 1.1 %copy-start.2 = (f32[9,8,17,128]{3,1,2,0:T(8,128)S(1)}, f32[9,8,17,128]{3,1,2,0:T(8,128)}, u32[]{:S(2)}) copy-start(f32[9,8,17,128]{3,1,2,0:T(8,128)} %copy.144) | copy-start | bytes 1880068
  68.2 4.9 %collective-permute-start.6 = (f32[58,13]{1,0:T(8,128)S(1)}, f32[58,13]{1,0:T(8,128)S(1)}, u32[]{:S(2)}, u32[]{:S(2)}) collective-permute-start(f32[58,13]{1,0:T(8,128)S(1)} %get-tuple-element.33), channel_id=1, source_target_pairs={{0,1},{2,3},{4,5},{6,7},{8,9},{10,11},{12,13},{14,15},{16,17},{18,... | collective-permute-start | bytes 9056 | tf_op jit(solution)/shard_map/ppermute | solution.py:16
  70.6 3.1 %collective-permute-start.7 = (f32[58,13]{1,0:T(8,128)S(1)}, f32[58,13]{1,0:T(8,128)S(1)}, u32[]{:S(2)}, u32[]{:S(2)}) collective-permute-start(f32[58,13]{1,0:T(8,128)S(1)} %get-tuple-element.32), channel_id=1, source_target_pairs={{1,0},{3,2},{5,4},{7,6},{9,8},{11,10},{13,12},{15,14},{17,16},{19,... | collective-permute-start | bytes 9056 | tf_op jit(solution)/shard_map/ppermute | solution.py:17
where the time goes:
time: 99.3 us; the launch traced here: 98.3 us
  matrix products  40.7 us (41%)
  starting transfers between devices  20.7 us (21%)
  local copies, waits for them, and re-layouts  16.1 us (16%)
  other arithmetic  10.5 us (11%)
  waiting for transfers between devices  4.59 us (5%)
  blocking collectives  4.15 us (4%)
  between operations  1.55 us (2%)
    dot_general x10, matrix products, horizontal(): jnp.einsum('rbi,oi->rbo', tiles[:, :blocks], main, precision=lax.Precisio...  14.7 us
    dot_general x10, matrix products, horizontal(): jnp.einsum('rbi,oi->rbo', tiles[:, 1:], carry, precision=lax.Precision.HI...  14.4 us
    ppermute x4, starting transfers between devices, with_halo(): before = lax.ppermute(last, axis, up)  13.6 us
    dot_general x10, matrix products, vertical(): return jnp.dot(matrix, field, precision=lax.Precision.HIGHEST)  11.7 us
    ppermute x4, starting transfers between devices, with_halo(): after = lax.ppermute(first, axis, down)  7.03 us
    unnamed x30, local copies, waits for them, and re-layouts  5.25 us
    slice x1, local copies, waits for them, and re-layouts, local(): coarse_base = top_level[0::2, 0::2]  4.39 us
    all_to_all x1, blocking collectives, local(): lax.all_to_all(stacked, 'col', split_axis=1, concat_axis=2, tiled=True)  4.15 us
  transfers between devices with their start and end apart: 8, of which 3 were waited for; matrix products, arithmetic and copies ran while one was open for 10% of the time, Pallas kernels for 0%

commit v1 on v0

v1 whole, which is shorter than its diff:
```python
import functools

import jax
import jax.numpy as jnp
import numpy as np
from jax import lax
from jax.experimental import pallas as pl
from jax.experimental.pallas import tpu as pltpu
from jax.sharding import PartitionSpec as P

SIGMAS = [1.6 * 2.0 ** (k / 4.0) for k in range(5)]
LEVELS = 5
LANE = 128
HALF = LANE // 2
RIM = 16
MESH = pl.DeviceIdType.MESH
BF = jnp.bfloat16
F32 = jnp.float32


def taps_at(sigma, offset):
    spread = np.arange(25, dtype=np.float64) - 12.0
    total = np.sum(np.exp(-spread * spread / (2.0 * sigma * sigma)))
    weight = np.exp(-(offset**2) / (2.0 * sigma * sigma)) / total
    return np.where(np.abs(offset) <= 12, weight, 0.0)


def halves(matrix):
    high = matrix.astype(BF)
    low = (matrix - high.astype(np.float64)).astype(BF)
    return high, low


def ring_rows(count):
    rows = np.full(count + 8, 10**6, dtype=np.float64)
    rows[: count + 1] = np.arange(count + 1)
    rows[-1] = -1
    return rows


def ring_inputs(count, before):
    total = np.arange(count, dtype=np.float64)
    return np.where(total >= count - before, total - count, total)


def vertical_matrix(out_rows, in_rows, sigma):
    return taps_at(sigma, in_rows[None, :] - out_rows[:, None])


def pad_rows(matrix, multiple):
    return np.pad(matrix, ((0, -matrix.shape[0] % multiple), (0, 0)))


def column_weights(matrix):
    high, low = halves(matrix)
    pair = np.concatenate([high, low], axis=1)
    return np.concatenate([pair, pair], axis=0)


def row_weights(matrix):
    high, low = halves(pad_rows(matrix, 16))
    return np.concatenate([high, high, low, low], axis=1)


def split(x):
    high = x.astype(BF)
    low = (x - high.astype(F32)).astype(BF)
    return high, low


def kernel(
    rows_total, image, a_fine, a_coarse, g_level, g_base,
    dog_fine, hess_fine, dog_coarse, hess_coarse,
    ext, cext, vert, lev, diff, base,
    load_sem, fsend, frecv, csend, crecv,
):
    tile_rows, tile_cols = image.shape
    tiles = tile_cols // LANE
    strip = tile_rows // 4
    half_cols = tile_cols // 2
    r = lax.axis_index("row")
    c = lax.axis_index("col")
    other = 1 - c
    has_up = r > 0
    has_down = r < rows_total - 1

    load = pltpu.make_async_copy(image, ext.at[pl.ds(0, tile_rows), pl.ds(0, tile_cols)], load_sem)
    load.start()

    barrier = pltpu.get_barrier_semaphore()

    def greet(row, col):
        pl.semaphore_signal(barrier, inc=1, device_id={"row": row, "col": col}, device_id_type=MESH)

    greet(r, other)

    @pl.when(has_up)
    def _():
        greet(r - 1, c)
        greet(r - 1, other)

    @pl.when(has_down)
    def _():
        greet(r + 1, c)
        greet(r + 1, other)

    ends = (r == 0).astype(jnp.int32) + (r == rows_total - 1).astype(jnp.int32)
    pl.semaphore_wait(barrier, 5 - 2 * ends)

    load.wait()

    def remote(src, dst, send, recv, row, col):
        return pltpu.make_async_remote_copy(
            src_ref=src, dst_ref=dst, send_sem=send, recv_sem=recv,
            device_id={"row": row, "col": col}, device_id_type=MESH,
        )

    edge = pl.ds(pl.multiple_of(other * (tile_cols - LANE), LANE), LANE)
    own = pl.ds(0, tile_cols)
    rim = pl.ds(tile_cols, LANE)
    first = pl.ds(0, RIM)
    last = pl.ds(tile_rows - RIM, RIM)
    below = pl.ds(tile_rows, RIM)
    above = pl.ds(tile_rows + RIM, RIM)
    inner = pl.ds(0, tile_rows)

    to_down = remote(ext.at[last, own], ext.at[above, own], fsend.at[0], frecv.at[0], r + 1, c)
    to_down_corner = remote(ext.at[last, edge], ext.at[above, rim], fsend.at[1], frecv.at[1], r + 1, other)
    to_up = remote(ext.at[first, own], ext.at[below, own], fsend.at[2], frecv.at[2], r - 1, c)
    to_up_corner = remote(ext.at[first, edge], ext.at[below, rim], fsend.at[3], frecv.at[3], r - 1, other)
    to_side = remote(ext.at[inner, edge], ext.at[inner, rim], fsend.at[4], frecv.at[4], r, other)

    @pl.when(has_down)
    def _():
        to_down.start()
        to_down_corner.start()

    @pl.when(has_up)
    def _():
        to_up.start()
        to_up_corner.start()

    to_side.start()

    wide = tile_cols + LANE

    @pl.when(r == 0)
    def _():
        ext[above, :] = jnp.zeros((RIM, wide), F32)

    @pl.when(r == rows_total - 1)
    def _():
        ext[below, :] = jnp.zeros((RIM, wide), F32)

    cext[:, pl.ds(tile_cols, LANE)] = jnp.zeros((3 * strip, LANE), F32)

    @pl.when(jnp.logical_and(r == 0, c == 0))
    def _():
        cext[pl.ds(2 * strip, strip), own] = jnp.zeros((strip, tile_cols), F32)

    @pl.when(jnp.logical_and(r == rows_total - 1, c == 1))
    def _():
        cext[pl.ds(strip, strip), own] = jnp.zeros((strip, tile_cols), F32)

    to_side.wait()

    @pl.when(has_up)
    def _():
        to_down.wait_recv()
        to_down_corner.wait_recv()

    @pl.when(has_down)
    def _():
        to_up.wait_recv()
        to_up_corner.wait_recv()

    lane = lax.broadcasted_iota(jnp.int32, (1, LANE), 1)

    def vertical_pass(source, matrix, edge_keep):
        def tile_of(t):
            value = source[:, t * LANE : (t + 1) * LANE]
            if t == tiles:
                value = value * edge_keep
            return pltpu.roll(value, HALF, 1)

        rolled = [tile_of(t) for t in range(tiles + 1)]
        left = lane < HALF
        for t0 in range(0, tiles + 1, 4):
            group = [
                jnp.where(left, rolled[t - 1], rolled[t])
                for t in range(t0, min(t0 + 4, tiles + 1))
            ]
            high, low = split(jnp.concatenate(group, axis=1))
            stacked = jnp.concatenate([high, low, high, low], axis=0)
            count = matrix.shape[0]
            vert[pl.ds(0, count), t0 * LANE : t0 * LANE + stacked.shape[1]] = jnp.dot(
                matrix[...], stacked, preferred_element_type=F32
            )

    keep = jnp.where((lane < HALF) == (c == 0), 1.0, 0.0).astype(F32)
    vertical_pass(ext, a_fine, keep)

    half_rows = tile_rows // 2
    windows = []
    for b in range(half_cols // LANE):
        windows.append(vert[0:half_rows, 2 * b * LANE : (2 * b + 3) * LANE])
    high, low = split(jnp.concatenate(windows, axis=0))
    product = jnp.dot(jnp.concatenate([high, low], axis=1), g_base[...], preferred_element_type=F32)
    product = product[:, :LANE] + product[:, LANE:]
    for b in range(half_cols // LANE):
        base[:, b * LANE : (b + 1) * LANE] = product[b * half_rows : (b + 1) * half_rows]

    mine = pl.ds(pl.multiple_of(c * half_cols, LANE), half_cols)
    top, bottom = base.at[pl.ds(0, strip)], base.at[pl.ds(strip, strip)]

    def slot(index):
        return cext.at[pl.ds(pl.multiple_of(index * strip, 8), strip), mine]

    sends = [
        remote(top, slot(2 * other), csend.at[0], crecv.at[0], r, other),
        remote(bottom, slot(c), csend.at[1], crecv.at[1], r, other),
    ]
    up = remote(top, slot(1), csend.at[2], crecv.at[2 + c], r - 1, 1)
    down = remote(bottom, slot(2), csend.at[3], crecv.at[2 + c], r + 1, 0)

    @pl.when(has_up)
    def _():
        up.start()

    @pl.when(has_down)
    def _():
        down.start()

    for send in sends:
        send.start()

    cext[pl.ds(pl.multiple_of(2 * c * strip, 8), strip), mine] = base[0:strip]
    cext[pl.ds(pl.multiple_of(other * strip, 8), strip), mine] = base[strip : 2 * strip]

    def horizontal_pass(start, high_rows, blocks):
        for k in range(LEVELS):
            rows = pl.ds(start + k * high_rows, high_rows)
            windows = []
            for b in range(blocks):
                if b == tiles:
                    windows.append(
                        jnp.concatenate([vert[rows, b * LANE : (b + 1) * LANE], vert[rows, 0:LANE]], axis=1)
                    )
                else:
                    windows.append(vert[rows, b * LANE : (b + 2) * LANE])
            high, low = split(jnp.concatenate(windows, axis=0))
            product = jnp.dot(
                jnp.concatenate([high, low], axis=1), g_level[k], preferred_element_type=F32
            )
            lev[k, pl.ds(0, blocks * high_rows), :] = product[:, :LANE] + product[:, LANE:]

    def responses(count, blocks, dog_gain, hess_gain, row_keep, edge_keep, dog, hess):
        high_rows = count + 8
        for b in range(blocks):
            rows = pl.ds(b * high_rows, high_rows)
            level = [lev[k, rows, :] for k in range(LEVELS)]
            for k in range(LEVELS - 1):
                d = level[k + 1] - level[k]
                if b < tiles:
                    dog[k, :, b * LANE : (b + 1) * LANE] = (dog_gain * d[:count]).astype(BF)
                if k in (1, 2):
                    d = d * row_keep
                    if b == tiles:
                        d = d * edge_keep
                    diff[k - 1, rows, :] = d
        if blocks == tiles:
            diff[:, pl.ds(tiles * high_rows, high_rows), :] = jnp.zeros((2, high_rows, LANE), F32)

        def block(b):
            before, after = (b - 1) % (tiles + 1), (b + 1) % (tiles + 1)
            for m in range(2):
                centre = diff[m, pl.ds(b * high_rows, high_rows), :]
                previous = diff[m, pl.ds(before * high_rows, high_rows), :]
                following = diff[m, pl.ds(after * high_rows, high_rows), :]
                right = pltpu.roll(jnp.where(lane == 0, following, centre), LANE - 1, 1)
                left = pltpu.roll(jnp.where(lane == LANE - 1, previous, centre), 1, 1)
                slope = right - left
                dxx = (right + left - 2.0 * centre)[:count]
                twice = 2.0 * centre
                dyy = (
                    pltpu.roll(centre, high_rows - 1, 0) + pltpu.roll(centre, 1, 0) - twice
                )[:count]
                dxy = (pltpu.roll(slope, high_rows - 1, 0) - pltpu.roll(slope, 1, 0))[:count] * 0.25
                hess[m, :, b * LANE : (b + 1) * LANE] = (hess_gain * (dxx * dyy - dxy * dxy)).astype(BF)

        for b in range(tiles):
            block(b)

    def row_mask(count, before, after):
        index = lax.broadcasted_iota(jnp.int32, (count + 8, 1), 0)
        gone = jnp.logical_or(
            jnp.logical_and(index == count, jnp.logical_not(after)),
            jnp.logical_and(index == count + 7, jnp.logical_not(before)),
        )
        return jnp.where(gone, 0.0, 1.0).astype(F32)

    horizontal_pass(half_rows, tile_rows + 8, tiles + 1)
    edge_keep = jnp.where(lane == jnp.where(c == 0, 0, LANE - 1), 1.0, 0.0).astype(F32)
    responses(
        tile_rows, tiles + 1, 20.0, 5000.0,
        row_mask(tile_rows, has_up, has_down), edge_keep, dog_fine, hess_fine,
    )

    for send in sends:
        send.wait_recv()

    @pl.when(jnp.logical_or(c == 1, has_up))
    def _():
        @pl.when(jnp.logical_or(c == 0, has_down))
        def _():
            for index in range(2):
                remote(top, slot(1), csend.at[2], crecv.at[2 + index], r, other).wait_recv()

    vertical_pass(cext, a_coarse, jnp.ones((1, LANE), F32))
    horizontal_pass(0, strip + 8, tiles)
    responses(
        strip, tiles, 80.0, 200000.0,
        row_mask(strip, jnp.logical_or(has_up, c == 1), jnp.logical_or(has_down, c == 0)),
        None, dog_coarse, hess_coarse,
    )

    @pl.when(has_down)
    def _():
        to_down.wait_send()
        to_down_corner.wait_send()
        down.wait_send()

    @pl.when(has_up)
    def _():
        to_up.wait_send()
        to_up_corner.wait_send()
        up.wait_send()

    for send in sends:
        send.wait_send()


def solution(mesh):
    rows_total = mesh.shape["row"]

    def local(image):
        tile_rows, tile_cols = image.shape
        strip = tile_rows // 4
        tiles = tile_cols // LANE
        fine_in = ring_inputs(tile_rows + 2 * RIM, RIM)
        coarse_in = ring_inputs(3 * strip, strip)
        a_fine = row_weights(
            np.concatenate(
                [vertical_matrix(2.0 * np.arange(tile_rows // 2), fine_in, SIGMAS[4])]
                + [vertical_matrix(ring_rows(tile_rows), fine_in, s) for s in SIGMAS]
            )
        )
        a_coarse = row_weights(
            np.concatenate([vertical_matrix(ring_rows(strip), coarse_in, s) for s in SIGMAS])
        )
        window = np.arange(2 * LANE, dtype=np.float64)[:, None] - HALF
        g_level = np.stack(
            [column_weights(taps_at(s, window - np.arange(LANE)[None, :])) for s in SIGMAS]
        )
        wider = np.arange(3 * LANE, dtype=np.float64)[:, None] - HALF
        g_base = column_weights(taps_at(SIGMAS[4], wider - 2.0 * np.arange(LANE)[None, :]))

        vmem = pl.BlockSpec(memory_space=pltpu.VMEM)
        ring = tile_rows + 8
        wide = tile_cols + LANE
        return pl.pallas_call(
            functools.partial(kernel, rows_total),
            out_shape=(
                jax.ShapeDtypeStruct((4, tile_rows, tile_cols), BF),
                jax.ShapeDtypeStruct((2, tile_rows, tile_cols), BF),
                jax.ShapeDtypeStruct((4, strip, tile_cols), BF),
                jax.ShapeDtypeStruct((2, strip, tile_cols), BF),
            ),
            in_specs=[pl.BlockSpec(memory_space=pl.ANY)] + [vmem] * 4,
            out_specs=(vmem,) * 4,
            scratch_shapes=[
                pltpu.VMEM((tile_rows + 2 * RIM, wide), F32),
                pltpu.VMEM((3 * strip, wide), F32),
                pltpu.VMEM((a_fine.shape[0], wide), F32),
                pltpu.VMEM((LEVELS, (tiles + 1) * ring, LANE), F32),
                pltpu.VMEM((2, (tiles + 1) * ring, LANE), F32),
                pltpu.VMEM((tile_rows // 2, tile_cols // 2), F32),
                pltpu.SemaphoreType.DMA,
                pltpu.SemaphoreType.DMA((5,)),
                pltpu.SemaphoreType.DMA((5,)),
                pltpu.SemaphoreType.DMA((4,)),
                pltpu.SemaphoreType.DMA((4,)),
            ],
            compiler_params=pltpu.CompilerParams(
                collective_id=0, has_side_effects=True, vmem_limit_bytes=48 * 2**20
            ),
        )(image, a_fine, a_coarse, g_level, g_base)

    return jax.shard_map(
        local,
        mesh=mesh,
        in_specs=(P(("slab", "row"), "col"),),
        out_specs=(
            P(None, ("slab", "row"), "col"),
            P(None, ("slab", "row"), "col"),
            P(None, ("slab", "row", "col"), None),
            P(None, ("slab", "row", "col"), None),
        ),
        check_vma=False,
    )
```

time: 99.3 us -> 26.4 us (0.27)
  matrix products: 40.7 us -> 0 us
  starting transfers between devices: 20.7 us -> 0 us
  Pallas kernels: 0 us -> 17.2 us
  other arithmetic: 10.5 us -> 0 us
  local copies, waits for them, and re-layouts: 16.1 us -> 8.27 us
  waiting for transfers between devices: 4.59 us -> 0 us
  blocking collectives: 4.15 us -> 0 us
    dot_general x30 -> x0, matrix products: 40.7 us -> none  [the longest x10 14.7 us: horizontal(): jnp.einsum('rbi,oi->rbo', tiles[:, :blocks], main, precision=lax.Precisio...]
    ppermute x8 -> x0, starting transfers between devices: 20.7 us -> none  [the longest x4 13.6 us: with_halo(): before = lax.ppermute(last, axis, up)]
    pallas_call x0 -> x1, Pallas kernels: none -> 17.2 us  [local(): pl.pallas_call(functools.partial(kernel, rows_total), out_shape=(jax.Shap...]
    slice x18 -> x0, local copies, waits for them, and re-layouts: 7.96 us -> none  [the longest x1 4.39 us: local(): coarse_base = top_level[0::2, 0::2]]
    ppermute x8 -> x0, waiting for transfers between devices: 4.59 us -> none  [the longest x4 2.72 us: with_halo(): before = lax.ppermute(last, axis, up)]
    all_to_all x1 -> x0, blocking collectives: 4.15 us -> none  [local(): lax.all_to_all(stacked, 'col', split_axis=1, concat_axis=2, tiled=True)]
    reduce_sum x5 -> x0, other arithmetic: 3.15 us -> none  [band(): total = jnp.sum(jnp.exp(-spread * spread / (2.0 * sigma * sigma)))]
    unnamed x30 -> x14, local copies, waits for them, and re-layouts: 5.25 us -> 8.27 us
  transfers between devices with their start and end apart: 8 -> 0, of which waited for: 3 -> 0; matrix products, arithmetic and copies ran while one was open for 10% -> 0% of each run, Pallas kernels for 0% -> 0%
where the time goes in v1:
time: 26.4 us; the launch traced here: 26.1 us
  Pallas kernels  17.2 us (65%)
  local copies, waits for them, and re-layouts  8.27 us (31%)
  between operations  0.65 us (2%)
    pallas_call x1, Pallas kernels, local(): pl.pallas_call(functools.partial(kernel, rows_total), out_shape=(jax.Shap...  17.2 us
    unnamed x14, local copies, waits for them, and re-layouts  8.27 us

profile of v1, /device:TPU:14, one launch (start us, length us, event | category | flops | bytes accessed | tf_op | source)
XLA Modules:
  0.0 26.1 jit_solution(1001065321376975914)
XLA Ops:
  0.6 0.0 copy-start
  0.6 1.3 %copy-done = bf16[5,512,256]{2,1,0:T(8,128)(2,1)S(1)} copy-done((bf16[5,512,256]{2,1,0:T(8,128)(2,1)S(1)}, bf16[5,512,256]{2,1,0:T(8,128)(2,1)}, u32[]{:S(2)}) %copy-start) | copy-done | bytes 1310744
  1.9 0.0 copy-start.1
  2.0 1.0 %copy-done.1 = f32[64,2048]{1,0:T(8,128)S(1)} copy-done((f32[64,2048]{1,0:T(8,128)S(1)}, f32[64,2048]{1,0:T(8,128)}, u32[]{:S(2)}) %copy-start.1) | copy-done | bytes 524312
  3.0 0.0 copy-start.2
  3.0 1.0 %copy-done.2 = bf16[768,256]{1,0:T(8,128)(2,1)S(1)} copy-done((bf16[768,256]{1,0:T(8,128)(2,1)S(1)}, bf16[768,256]{1,0:T(8,128)(2,1)}, u32[]{:S(2)}) %copy-start.2) | copy-done | bytes 393240
  4.0 0.0 copy-start.3
  4.0 1.0 %copy-done.3 = bf16[400,384]{1,0:T(8,128)(2,1)S(1)} copy-done((bf16[400,384]{1,0:T(8,128)(2,1)S(1)}, bf16[400,384]{1,0:T(8,128)(2,1)}, u32[]{:S(2)}) %copy-start.3) | copy-done | bytes 307224
  5.0 0.0 copy-start.4
  5.0 0.8 %copy-done.4 = bf16[128,192]{1,0:T(8,128)(2,1)S(1)} copy-done((bf16[128,192]{1,0:T(8,128)(2,1)S(1)}, bf16[128,192]{1,0:T(8,128)(2,1)}, u32[]{:S(2)}) %copy-start.4) | copy-done | bytes 49176
  5.8 17.2 %shard_map.84 = (bf16[4,64,2048]{2,1,0:T(8,128)(2,1)S(1)}, bf16[2,64,2048]{2,1,0:T(8,128)(2,1)S(1)}, bf16[4,16,2048]{2,1,0:T(8,128)(2,1)S(1)}, bf16[2,16,2048]{2,1,0:T(8,128)(2,1)S(1)}) custom-call(f32[64,2048]{1,0:T(8,128)S(1)} %copy-done.1, bf16[400,384]{1,0:T(8,128)(2,1)S(1)} %copy-done.3, bf16[128,192]{1,0:T(8,128)(2,1)S(1)} %copy-done.4, ...), custom_call_target="tpu_custom_call" | custom-call | tf_op jit(solution)/shard_map/pallas_call | solution.py:371
  23.0 1.0 %copy.13 = bf16[4,64,2048]{2,1,0:T(8,128)(2,1)} copy(bf16[4,64,2048]{2,1,0:T(8,128)(2,1)S(1)} %get-tuple-element.8) | data formatting | bytes 2097152
  24.0 0.8 %copy.14 = bf16[2,64,2048]{2,1,0:T(8,128)(2,1)} copy(bf16[2,64,2048]{2,1,0:T(8,128)(2,1)S(1)} %get-tuple-element.9) | data formatting | bytes 1048576
  24.8 0.7 %copy.15 = bf16[4,16,2048]{2,1,0:T(8,128)(2,1)} copy(bf16[4,16,2048]{2,1,0:T(8,128)(2,1)S(1)} %get-tuple-element.10) | data formatting | bytes 524288
  25.5 0.7 %copy.16 = bf16[2,16,2048]{2,1,0:T(8,128)(2,1)} copy(bf16[2,16,2048]{2,1,0:T(8,128)(2,1)S(1)} %get-tuple-element.11) | data formatting | bytes 262144
Async XLA Ops:
  0.6 1.3 %copy-start = (bf16[5,512,256]{2,1,0:T(8,128)(2,1)S(1)}, bf16[5,512,256]{2,1,0:T(8,128)(2,1)}, u32[]{:S(2)}) copy-start(bf16[5,512,256]{2,1,0:T(8,128)(2,1)} %constant.10.clone.g_level) | copy-start | bytes 3932164
  1.9 1.0 %copy-start.1 = (f32[64,2048]{1,0:T(8,128)S(1)}, f32[64,2048]{1,0:T(8,128)}, u32[]{:S(2)}) copy-start(f32[64,2048]{1,0:T(8,128)} %image.1) | copy-start | bytes 1572868
  3.0 1.0 %copy-start.2 = (bf16[768,256]{1,0:T(8,128)(2,1)S(1)}, bf16[768,256]{1,0:T(8,128)(2,1)}, u32[]{:S(2)}) copy-start(bf16[768,256]{1,0:T(8,128)(2,1)} %constant.11.clone.g_base) | copy-start | bytes 1179652
  4.0 1.0 %copy-start.3 = (bf16[400,384]{1,0:T(8,128)(2,1)S(1)}, bf16[400,384]{1,0:T(8,128)(2,1)}, u32[]{:S(2)}) copy-start(bf16[400,384]{1,0:T(8,128)(2,1)} %constant.8.clone.a_fine) | copy-start | bytes 921604
  5.0 0.8 %copy-start.4 = (bf16[128,192]{1,0:T(8,128)(2,1)S(1)}, bf16[128,192]{1,0:T(8,128)(2,1)}, u32[]{:S(2)}) copy-start(bf16[128,192]{1,0:T(8,128)(2,1)} %constant.9.clone.a_coarse) | copy-start | bytes 147460

commit v2 on v1

--- a/solution.py
+++ b/solution.py
@@ -13,6 +13,7 @@
 LANE = 128
 HALF = LANE // 2
 RIM = 16
+CHUNK = 4
 MESH = pl.DeviceIdType.MESH
 BF = jnp.bfloat16
 F32 = jnp.float32
@@ -69,9 +70,9 @@
 
 
 def kernel(
-    rows_total, image, a_fine, a_coarse, g_level, g_base,
+    rows_total, image, a_fine_far, a_coarse_far, g_level_far, g_base_far,
     dog_fine, hess_fine, dog_coarse, hess_coarse,
-    ext, cext, vert, lev, diff, base,
+    ext, cext, vert, lev, diff, base, a_fine, a_coarse, g_level, g_base,
     load_sem, fsend, frecv, csend, crecv,
 ):
     tile_rows, tile_cols = image.shape
@@ -84,8 +85,12 @@
     has_up = r > 0
     has_down = r < rows_total - 1
 
-    load = pltpu.make_async_copy(image, ext.at[pl.ds(0, tile_rows), pl.ds(0, tile_cols)], load_sem)
+    load = pltpu.make_async_copy(image, ext.at[pl.ds(0, tile_rows), pl.ds(0, tile_cols)], load_sem.at[0])
     load.start()
+    pairs = [(a_fine_far, a_fine), (g_base_far, g_base), (g_level_far, g_level), (a_coarse_far, a_coarse)]
+    weights = [
+        pltpu.make_async_copy(far, near, load_sem.at[1 + i]) for i, (far, near) in enumerate(pairs)
+    ]
 
     barrier = pltpu.get_barrier_semaphore()
 
@@ -107,6 +112,8 @@
     ends = (r == 0).astype(jnp.int32) + (r == rows_total - 1).astype(jnp.int32)
     pl.semaphore_wait(barrier, 5 - 2 * ends)
 
+    for weight in weights:
+        weight.start()
     load.wait()
 
     def remote(src, dst, send, recv, row, col):
@@ -124,21 +131,35 @@
     above = pl.ds(tile_rows + RIM, RIM)
     inner = pl.ds(0, tile_rows)
 
-    to_down = remote(ext.at[last, own], ext.at[above, own], fsend.at[0], frecv.at[0], r + 1, c)
-    to_down_corner = remote(ext.at[last, edge], ext.at[above, rim], fsend.at[1], frecv.at[1], r + 1, other)
-    to_up = remote(ext.at[first, own], ext.at[below, own], fsend.at[2], frecv.at[2], r - 1, c)
-    to_up_corner = remote(ext.at[first, edge], ext.at[below, rim], fsend.at[3], frecv.at[3], r - 1, other)
-    to_side = remote(ext.at[inner, edge], ext.at[inner, rim], fsend.at[4], frecv.at[4], r, other)
+    chunks = tiles // CHUNK
+    span = CHUNK * LANE
+    to_down, to_up = [], []
+    for j in range(chunks):
+        part = pl.ds(j * span, span)
+        to_down.append(remote(ext.at[last, part], ext.at[above, part], fsend.at[2 * j], frecv.at[2 * j], r + 1, c))
+        to_up.append(
+            remote(ext.at[first, part], ext.at[below, part], fsend.at[2 * j + 1], frecv.at[2 * j + 1], r - 1, c)
+        )
+    n = 2 * chunks
+    to_down_corner = remote(ext.at[last, edge], ext.at[above, rim], fsend.at[n], frecv.at[n], r + 1, other)
+    to_up_corner = remote(ext.at[first, edge], ext.at[below, rim], fsend.at[n + 1], frecv.at[n + 1], r - 1, other)
+    to_side = remote(ext.at[inner, edge], ext.at[inner, rim], fsend.at[n + 2], frecv.at[n + 2], r, other)
 
     @pl.when(has_down)
     def _():
-        to_down.start()
         to_down_corner.start()
+        to_down[0].start()
 
     @pl.when(has_up)
     def _():
-        to_up.start()
         to_up_corner.start()
+        for send in to_up:
+            send.start()
+
+    @pl.when(has_down)
+    def _():
+        for send in to_down[1:]:
+            send.start()
 
     to_side.start()
 
@@ -162,86 +183,41 @@
     def _():
         cext[pl.ds(strip, strip), own] = jnp.zeros((strip, tile_cols), F32)
 
+    for weight in weights:
+        weight.wait()
     to_side.wait()
 
     @pl.when(has_up)
     def _():
-        to_down.wait_recv()
         to_down_corner.wait_recv()
 
     @pl.when(has_down)
     def _():
-        to_up.wait_recv()
         to_up_corner.wait_recv()
 
     lane = lax.broadcasted_iota(jnp.int32, (1, LANE), 1)
 
-    def vertical_pass(source, matrix, edge_keep):
+    def vertical_pass(source, matrix, edge_keep, begin, end):
         def tile_of(t):
             value = source[:, t * LANE : (t + 1) * LANE]
             if t == tiles:
                 value = value * edge_keep
             return pltpu.roll(value, HALF, 1)
 
-        rolled = [tile_of(t) for t in range(tiles + 1)]
+        rolled = {t: tile_of(t % (tiles + 1)) for t in range(begin - 1, end)}
         left = lane < HALF
-        for t0 in range(0, tiles + 1, 4):
-            group = [
-                jnp.where(left, rolled[t - 1], rolled[t])
-                for t in range(t0, min(t0 + 4, tiles + 1))
-            ]
-            high, low = split(jnp.concatenate(group, axis=1))
-            stacked = jnp.concatenate([high, low, high, low], axis=0)
-            count = matrix.shape[0]
-            vert[pl.ds(0, count), t0 * LANE : t0 * LANE + stacked.shape[1]] = jnp.dot(
-                matrix[...], stacked, preferred_element_type=F32
-            )
-
-    keep = jnp.where((lane < HALF) == (c == 0), 1.0, 0.0).astype(F32)
-    vertical_pass(ext, a_fine, keep)
-
-    half_rows = tile_rows // 2
-    windows = []
-    for b in range(half_cols // LANE):
-        windows.append(vert[0:half_rows, 2 * b * LANE : (2 * b + 3) * LANE])
-    high, low = split(jnp.concatenate(windows, axis=0))
-    product = jnp.dot(jnp.concatenate([high, low], axis=1), g_base[...], preferred_element_type=F32)
-    product = product[:, :LANE] + product[:, LANE:]
-    for b in range(half_cols // LANE):
-        base[:, b * LANE : (b + 1) * LANE] = product[b * half_rows : (b + 1) * half_rows]
-
-    mine = pl.ds(pl.multiple_of(c * half_cols, LANE), half_cols)
-    top, bottom = base.at[pl.ds(0, strip)], base.at[pl.ds(strip, strip)]
-
-    def slot(index):
-        return cext.at[pl.ds(pl.multiple_of(index * strip, 8), strip), mine]
-
-    sends = [
-        remote(top, slot(2 * other), csend.at[0], crecv.at[0], r, other),
-        remote(bottom, slot(c), csend.at[1], crecv.at[1], r, other),
-    ]
-    up = remote(top, slot(1), csend.at[2], crecv.at[2 + c], r - 1, 1)
-    down = remote(bottom, slot(2), csend.at[3], crecv.at[2 + c], r + 1, 0)
-
-    @pl.when(has_up)
-    def _():
-        up.start()
-
-    @pl.when(has_down)
-    def _():
-        down.start()
-
-    for send in sends:
-        send.start()
-
-    cext[pl.ds(pl.multiple_of(2 * c * strip, 8), strip), mine] = base[0:strip]
-    cext[pl.ds(pl.multiple_of(other * strip, 8), strip), mine] = base[strip : 2 * strip]
-
-    def horizontal_pass(start, high_rows, blocks):
+        group = [jnp.where(left, rolled[t - 1], rolled[t]) for t in range(begin, end)]
+        high, low = split(jnp.concatenate(group, axis=1))
+        stacked = jnp.concatenate([high, low, high, low], axis=0)
+        vert[pl.ds(0, matrix.shape[0]), begin * LANE : end * LANE] = jnp.dot(
+            matrix[...], stacked, preferred_element_type=F32
+        )
+
+    def horizontal_pass(start, high_rows, begin, end):
         for k in range(LEVELS):
             rows = pl.ds(start + k * high_rows, high_rows)
             windows = []
-            for b in range(blocks):
+            for b in range(begin, end):
                 if b == tiles:
                     windows.append(
                         jnp.concatenate([vert[rows, b * LANE : (b + 1) * LANE], vert[rows, 0:LANE]], axis=1)
@@ -252,7 +228,79 @@
             product = jnp.dot(
                 jnp.concatenate([high, low], axis=1), g_level[k], preferred_element_type=F32
             )
-            lev[k, pl.ds(0, blocks * high_rows), :] = product[:, :LANE] + product[:, LANE:]
+            lev[k, pl.ds(begin * high_rows, (end - begin) * high_rows), :] = (
+                product[:, :LANE] + product[:, LANE:]
+            )
+
+    half_rows = tile_rows // 2
+
+    def base_pass(begin, end):
+        windows = [vert[0:half_rows, 2 * b * LANE : (2 * b + 3) * LANE] for b in range(begin, end)]
+        high, low = split(jnp.concatenate(windows, axis=0))
+        product = jnp.dot(
+            jnp.concatenate([high, low], axis=1), g_base[...], preferred_element_type=F32
+        )
+        product = product[:, :LANE] + product[:, LANE:]
+        for b in range(begin, end):
+            base[:, b * LANE : (b + 1) * LANE] = product[
+                (b - begin) * half_rows : (b - begin + 1) * half_rows
+            ]
+
+    keep = jnp.where((lane < HALF) == (c == 0), 1.0, 0.0).astype(F32)
+    sends, ups, downs = [], [], []
+    base_done = 0
+    blocks_done = 0
+    for j in range(chunks):
+
+        @pl.when(has_up)
+        def _():
+            to_down[j].wait_recv()
+
+        @pl.when(has_down)
+        def _():
+            to_up[j].wait_recv()
+
+        ready = CHUNK * (j + 1) + (1 if j == chunks - 1 else 0)
+        vertical_pass(ext, a_fine, keep, CHUNK * j, ready)
+        base_end = (ready - 1) // 2
+        base_pass(base_done, base_end)
+
+        near = pl.ds(base_done * LANE, (base_end - base_done) * LANE)
+        mine = pl.ds(
+            pl.multiple_of(c * half_cols + base_done * LANE, LANE), (base_end - base_done) * LANE
+        )
+        top, bottom = base.at[pl.ds(0, strip), near], base.at[pl.ds(strip, strip), near]
+
+        def slot_rows(index):
+            return pl.ds(pl.multiple_of(index * strip, 8), strip)
+
+        pair = [
+            remote(top, cext.at[slot_rows(2 * other), mine], csend.at[4 * j], crecv.at[4 * j], r, other),
+            remote(bottom, cext.at[slot_rows(c), mine], csend.at[4 * j + 1], crecv.at[4 * j + 1], r, other),
+        ]
+        up = remote(top, cext.at[slot_rows(1), mine], csend.at[4 * j + 2], crecv.at[4 * j + 2 + c], r - 1, 1)
+        down = remote(bottom, cext.at[slot_rows(2), mine], csend.at[4 * j + 3], crecv.at[4 * j + 2 + c], r + 1, 0)
+        sends += pair
+        ups.append(up)
+        downs.append(down)
+
+        @pl.when(has_up)
+        def _():
+            up.start()
+
+        @pl.when(has_down)
+        def _():
+            down.start()
+
+        for send in pair:
+            send.start()
+
+        cext[slot_rows(2 * c), mine] = base[0:strip, near]
+        cext[slot_rows(other), mine] = base[strip : 2 * strip, near]
+
+        blocks_end = tiles + 1 if j == chunks - 1 else ready - 1
+        horizontal_pass(half_rows, tile_rows + 8, blocks_done, blocks_end)
+        base_done, blocks_done = base_end, blocks_end
 
     def responses(count, blocks, dog_gain, hess_gain, row_keep, edge_keep, dog, hess):
         high_rows = count + 8
@@ -299,7 +347,6 @@
         )
         return jnp.where(gone, 0.0, 1.0).astype(F32)
 
-    horizontal_pass(half_rows, tile_rows + 8, tiles + 1)
     edge_keep = jnp.where(lane == jnp.where(c == 0, 0, LANE - 1), 1.0, 0.0).astype(F32)
     responses(
         tile_rows, tiles + 1, 20.0, 5000.0,
@@ -313,11 +360,18 @@
     def _():
         @pl.when(jnp.logical_or(c == 0, has_down))
         def _():
-            for index in range(2):
-                remote(top, slot(1), csend.at[2], crecv.at[2 + index], r, other).wait_recv()
-
-    vertical_pass(cext, a_coarse, jnp.ones((1, LANE), F32))
-    horizontal_pass(0, strip + 8, tiles)
+            for j in range(chunks):
+                for index in range(2):
+                    pltpu.make_async_remote_copy(
+                        src_ref=ups[j].src_ref, dst_ref=ups[j].dst_ref,
+                        send_sem=csend.at[4 * j + 2], recv_sem=crecv.at[4 * j + 2 + index],
+                        device_id={"row": r, "col": other}, device_id_type=MESH,
+                    ).wait_recv()
+
+    for begin in range(0, tiles, CHUNK):
+        end = begin + CHUNK + (1 if begin + CHUNK == tiles else 0)
+        vertical_pass(cext, a_coarse, jnp.ones((1, LANE), F32), begin, end)
+    horizontal_pass(0, strip + 8, 0, tiles)
     responses(
         strip, tiles, 80.0, 200000.0,
         row_mask(strip, jnp.logical_or(has_up, c == 1), jnp.logical_or(has_down, c == 0)),
@@ -326,15 +380,15 @@
 
     @pl.when(has_down)
     def _():
-        to_down.wait_send()
         to_down_corner.wait_send()
-        down.wait_send()
+        for send in to_down + downs:
+            send.wait_send()
 
     @pl.when(has_up)
     def _():
-        to_up.wait_send()
         to_up_corner.wait_send()
-        up.wait_send()
+        for send in to_up + ups:
+            send.wait_send()
 
     for send in sends:
         send.wait_send()
@@ -368,6 +422,7 @@
         vmem = pl.BlockSpec(memory_space=pltpu.VMEM)
         ring = tile_rows + 8
         wide = tile_cols + LANE
+        chunks = tiles // CHUNK
         return pl.pallas_call(
             functools.partial(kernel, rows_total),
             out_shape=(
@@ -376,7 +431,7 @@
                 jax.ShapeDtypeStruct((4, strip, tile_cols), BF),
                 jax.ShapeDtypeStruct((2, strip, tile_cols), BF),
             ),
-            in_specs=[pl.BlockSpec(memory_space=pl.ANY)] + [vmem] * 4,
+            in_specs=[pl.BlockSpec(memory_space=pltpu.HBM)] * 5,
             out_specs=(vmem,) * 4,
             scratch_shapes=[
                 pltpu.VMEM((tile_rows + 2 * RIM, wide), F32),
@@ -385,14 +440,18 @@
                 pltpu.VMEM((LEVELS, (tiles + 1) * ring, LANE), F32),
                 pltpu.VMEM((2, (tiles + 1) * ring, LANE), F32),
                 pltpu.VMEM((tile_rows // 2, tile_cols // 2), F32),
-                pltpu.SemaphoreType.DMA,
+                pltpu.VMEM(a_fine.shape, BF),
+                pltpu.VMEM(a_coarse.shape, BF),
+                pltpu.VMEM(g_level.shape, BF),
+                pltpu.VMEM(g_base.shape, BF),
                 pltpu.SemaphoreType.DMA((5,)),
-                pltpu.SemaphoreType.DMA((5,)),
-                pltpu.SemaphoreType.DMA((4,)),
-                pltpu.SemaphoreType.DMA((4,)),
+                pltpu.SemaphoreType.DMA((2 * chunks + 3,)),
+                pltpu.SemaphoreType.DMA((2 * chunks + 3,)),
+                pltpu.SemaphoreType.DMA((4 * chunks,)),
+                pltpu.SemaphoreType.DMA((4 * chunks,)),
             ],
             compiler_params=pltpu.CompilerParams(
-                collective_id=0, has_side_effects=True, vmem_limit_bytes=48 * 2**20
+                collective_id=0, has_side_effects=True, vmem_limit_bytes=62500000
             ),
         )(image, a_fine, a_coarse, g_level, g_base)
 

time: 26.4 us -> 24.3 us (0.920)
  the two profiles are of different devices: /device:TPU:14 before, /device:TPU:1 now
where the time goes in v2:
time: 24.3 us; the launch traced here: 24.1 us
  Pallas kernels  18.9 us (78%)
  local copies, waits for them, and re-layouts  4.54 us (19%)
  between operations  0.66 us (3%)
    pallas_call x1, Pallas kernels, local(): pl.pallas_call(functools.partial(kernel, rows_total), out_shape=(jax.Shap...  18.9 us
    unnamed x10, local copies, waits for them, and re-layouts  4.54 us

profile of v2, /device:TPU:1, one launch (start us, length us, event | category | flops | bytes accessed | tf_op | source)
XLA Modules:
  0.0 24.1 jit_solution(9809407781292647028)
XLA Ops:
  0.6 18.9 %shard_map.84 = (bf16[4,64,2048]{2,1,0:T(8,128)(2,1)}, bf16[2,64,2048]{2,1,0:T(8,128)(2,1)}, bf16[4,16,2048]{2,1,0:T(8,128)(2,1)}, bf16[2,16,2048]{2,1,0:T(8,128)(2,1)}) custom-call(f32[64,2048]{1,0:T(8,128)} %image.1, bf16[400,384]{1,0:T(8,128)(2,1)} %constant.8.clone.a_fine_far, bf16[128,192]{1,0:T(8,128)(2,1)} %constant.9.clone.a_coarse_far, ...), custom_call_target="tpu_custom_call" | custom-call | tf_op jit(solution)/shard_map/pallas_call | solution.py:426
  19.5 0.0 copy-start
  19.6 0.0 copy-start.1
  19.6 0.0 copy-start.2
  19.6 2.4 %copy.13 = bf16[4,64,2048]{2,1,0:T(8,128)(2,1)} copy(bf16[4,64,2048]{2,1,0:T(8,128)(2,1)} %get-tuple-element.8) | data formatting | bytes 2097152
  22.0 0.0 copy-done
  22.0 0.8 %copy.14 = bf16[2,64,2048]{2,1,0:T(8,128)(2,1)} copy(bf16[2,64,2048]{2,1,0:T(8,128)(2,1)S(1)} %copy-done) | data formatting | bytes 1048576
  22.8 0.0 copy-done.1
  22.8 0.7 %copy.15 = bf16[4,16,2048]{2,1,0:T(8,128)(2,1)} copy(bf16[4,16,2048]{2,1,0:T(8,128)(2,1)S(1)} %copy-done.1) | data formatting | bytes 524288
  23.5 0.0 copy-done.2
  23.5 0.7 %copy.16 = bf16[2,16,2048]{2,1,0:T(8,128)(2,1)} copy(bf16[2,16,2048]{2,1,0:T(8,128)(2,1)S(1)} %copy-done.2) | data formatting | bytes 262144
Async XLA Ops:
  19.5 2.4 %copy-start = (bf16[2,64,2048]{2,1,0:T(8,128)(2,1)S(1)}, bf16[2,64,2048]{2,1,0:T(8,128)(2,1)}, u32[]{:S(2)}) copy-start(bf16[2,64,2048]{2,1,0:T(8,128)(2,1)} %get-tuple-element.9) | copy-start | bytes 1572868
  19.6 3.2 %copy-start.1 = (bf16[4,16,2048]{2,1,0:T(8,128)(2,1)S(1)}, bf16[4,16,2048]{2,1,0:T(8,128)(2,1)}, u32[]{:S(2)}) copy-start(bf16[4,16,2048]{2,1,0:T(8,128)(2,1)} %get-tuple-element.10) | copy-start | bytes 786436
  19.6 3.9 %copy-start.2 = (bf16[2,16,2048]{2,1,0:T(8,128)(2,1)S(1)}, bf16[2,16,2048]{2,1,0:T(8,128)(2,1)}, u32[]{:S(2)}) copy-start(bf16[2,16,2048]{2,1,0:T(8,128)(2,1)} %get-tuple-element.11) | copy-start | bytes 393220
